TPU v7x, 32 devices: a 4x4x1 block of a 4x4x8 slice. The times are simulated.
32 devices in a mesh: dp: 2 (over z, core), tp: 16 (over x, y).
Axes of the slice: x: 4, y: 4, z: 1, core: 2. Of those that a mesh axis runs over, the one named last changes fastest.
The devices are a block of a 4x4x8 slice.
Arguments:
- x: bfloat16 [11264, 3072], P(('dp', 'tp')), parts along dimension 0
- w_gate: bfloat16 [3072, 24576], P(None, 'tp')
- w_up: bfloat16 [3072, 24576], P(None, 'tp')
- w_down: bfloat16 [24576, 3072], P('tp')
Outputs:
- output: bfloat16 [11264, 3072], P(('dp', 'tp')), parts along dimension 0
There are 2 independent parts. A program takes and returns all parts, laid end to end along the dimension named above; an argument that names none is the same for every part.
All inputs are finite; a program needn't handle non-finite values.
Results may differ from a plain program's by a relative error of at most 0.016.
Values are sent between devices in bfloat16 or wider.
A program may use at most 768 MiB of HBM per device.

v0:
```python
import jax
import jax.numpy as jnp
from jax import lax
from jax.sharding import PartitionSpec as P


def solution(mesh):
    def step(x, w_gate, w_up, w_down):
        rows = lax.all_gather(x, "tp", axis=0, tiled=True)
        gate = jnp.dot(rows, w_gate, preferred_element_type=jnp.float32)
        up = jnp.dot(rows, w_up, preferred_element_type=jnp.float32)
        hidden = (jax.nn.gelu(gate) * up).astype(jnp.bfloat16)
        term = jnp.dot(hidden, w_down, preferred_element_type=jnp.float32).astype(jnp.bfloat16)
        return lax.psum_scatter(term, "tp", scatter_dimension=0, tiled=True)

    return jax.shard_map(
        step,
        mesh=mesh,
        in_specs=(P(("dp", "tp"), None), P(None, "tp"), P(None, "tp"), P("tp", None)),
        out_specs=P(("dp", "tp"), None),
        check_vma=False,
    )
```

profile of v0, /device:TPU:97, one launch (start us, length us, event | category | flops | bytes accessed | tf_op | source)
XLA Modules:
  0.0 601.7 jit_solution(4406508842653634424)
XLA Ops:
  6.5 0.0 all-gather.2.cloned.1.call-start
  6.6 0.7 all-gather.2.cloned.1.call-update
  7.3 0.1 reduce-scatter.2.cloned.1.call-start
  7.4 202.8 %all-gather.2.cloned.1.call-done = bf16[5632,3072]{1,0:T(8,128)(2,1)} async-done(((bf16[352,3072]{1,0:T(8,128)(2,1)}), bf16[5632,3072]{1,0:T(8,128)(2,1)}) %all-gather.2.cloned.1.call-update) | async-done | bytes 34603024 | tf_op jit(solution)/shard_map/all_gather | solution.py:9
  210.2 0.0 copy-start
  210.2 63.6 %fusion.13 = f32[5632,1536]{1,0:T(8,128)} fusion(bf16[5632,3072]{1,0:T(8,128)(2,1)} %all-gather.2.cloned.1.call-done, bf16[3072,1536]{1,0:T(8,128)(2,1)} %param.5), kind=kOutput, calls=%fused_computation.15 | convolution fusion | flops 53150220288 | bytes 78643200 | tf_op jit(solution)/shard_map/dot_general | solution.py:10
  273.8 0.0 copy-done
  273.8 65.1 %fusion.8.clone.4 = bf16[5632,1536]{1,0:T(8,128)(2,1)} fusion(f32[5632,1536]{1,0:T(8,128)} %fusion.13, bf16[5632,3072]{1,0:T(8,128)(2,1)} %all-gather.2.cloned.1.call-done, bf16[3072,1536]{1,0:T(8,128)(2,1)S(1)} %copy-done), kind=kOutput, calls=%fused_computation.9.clone.clone.clone.1 | convolution fusion | flops 53236727808 | bytes 95944704 | tf_op jit(solution)/shard_map/dot_general | solution.py:11
  338.9 61.3 %convolution_convert_fusion = bf16[5632,3072]{1,0:T(8,128)(2,1)} fusion(bf16[1536,3072]{1,0:T(8,128)(2,1)} %param.7, bf16[5632,1536]{1,0:T(8,128)(2,1)} %fusion.8.clone.4), kind=kOutput, calls=%fused_computation.10 | convolution fusion | flops 53167521792 | bytes 61341696 | tf_op jit(solution)/shard_map/dot_general | solution.py:13
  400.2 0.1 reduce-scatter.2.cloned.1.call-update
  400.3 194.6 %reduce-scatter.2.cloned.1.call-done = bf16[352,3072]{1,0:T(8,128)(2,1)} async-done(((bf16[5632,3072]{1,0:T(8,128)(2,1)}), bf16[352,3072]{1,0:T(8,128)(2,1)}) %reduce-scatter.2.cloned.1.call-update) | async-done | bytes 2162704 | tf_op jit(solution)/shard_map/reduce_scatter | solution.py:14
Async XLA Ops:
  6.5 203.7 %all-gather.2.cloned.1.call-start = ((), (), s32[]{:S(2)}) async-start(), calls=%async_computation.1 | async-start | bytes 36765696 | tf_op jit(solution)/shard_map/all_gather | solution.py:9
  7.3 587.5 %reduce-scatter.2.cloned.1.call-start = ((), (), s32[]{:S(2)}) async-start(), calls=%async_computation.2 | async-start | bytes 36765696 | tf_op jit(solution)/shard_map/reduce_scatter | solution.py:14
  210.2 63.6 %copy-start = (bf16[3072,1536]{1,0:T(8,128)(2,1)S(1)}, bf16[3072,1536]{1,0:T(8,128)(2,1)}, u32[]{:S(2)}) copy-start(bf16[3072,1536]{1,0:T(8,128)(2,1)} %param.6) | copy-start | bytes 28311556
Sparse Core Ops, SparseCore 0:
  9.3 200.8 all-gather.1
  400.4 194.3 reduce-scatter.1
where the time goes:
time: 602 us
  waiting for transfers between devices  398 us (66%)
  matrix products  190 us (32%)
  between operations  13.4 us (2%)
    all_gather x1, waiting for transfers between devices, step(): rows = lax.all_gather(x, 'tp', axis=0, tiled=True)  203 us
    reduce_scatter x1, waiting for transfers between devices, step(): return lax.psum_scatter(term, 'tp', scatter_dimension=0, tiled=True)  195 us
    dot_general x1, matrix products, step(): up = jnp.dot(rows, w_up, preferred_element_type=jnp.float32)  65.1 us
    dot_general x1, matrix products, step(): gate = jnp.dot(rows, w_gate, preferred_element_type=jnp.float32)  63.6 us
    dot_general x1, matrix products, step(): jnp.dot(hidden, w_down, preferred_element_type=jnp.float32)  61.3 us
  transfers between devices with their start and end apart: 2, of which 2 were waited for; matrix products, arithmetic and copies ran while one was open for 0% of the time, Pallas kernels for 0%

commit v1 on v0

v1 whole, which is shorter than its diff:
```python
import functools
import math

import jax
import jax.numpy as jnp
from jax import lax
from jax.experimental import pallas as pl
from jax.experimental.pallas import tpu as pltpu
from jax.sharding import PartitionSpec as P

MESH = pl.DeviceIdType.MESH
TILE = 256
STAGE = 5
LOADS = 3
STAGE_MORE = 11

HALF_US, HOP_US, GATE_US, DOWN_US, LOAD_US = 23.6, 2.0, 8.6, 2.6, 2.0

BLOCKS = [
    (0, 0), (1, 0), (-1, 0), (0, 1), (0, -1), (1, 1), (1, -1), (-1, 1), (-1, -1),
    (2, 0), (0, 2), (2, 1), (1, 2), (2, -1), (-1, 2), (2, 2),
]
SLOT = {b: i for i, b in enumerate(BLOCKS)}
COL = {1: 0, -1: 1}


def norm(o):
    return (o + 1) % 4 - 1


def place(h, first, second):
    a, b = norm(first), norm(second)
    return SLOT[(a, b) if h == 0 else (b, a)]


def gather_plan():
    plan = {}
    for h in (0, 1):
        f, s = h, 1 - h
        for d in (1, -1):
            plan["g1", h, d] = (f, d, 1.0, place(h, 0, 0), place(h, -d, 0), h, None, [])
        for d in (1, -1):
            for o in (0, -1, 1):
                needs = [("g1", h, -o)] if o else []
                plan["g3", h, o, d] = (s, d, 1.0, place(h, o, 0), place(h, o, -d), h, None, needs)
        for d in (1, -1):
            plan["g2", h, d] = (f, d, 0.5, place(h, -d, 0), place(h, 2, 0), h, COL[d], [("g1", h, d)])
        for d in (1, -1):
            for e in (1, -1):
                plan["g3", h, 2, e, d] = (
                    s, d, 0.5, place(h, 2, 0), place(h, 2, -d), h, COL[e], [("g2", h, e)],
                )
            for o in (0, -1, 1):
                plan["g4", h, o, d] = (
                    s, d, 0.5, place(h, o, -d), place(h, o, 2), h, COL[d], [("g3", h, o, d)],
                )
            plan["g4", h, 2, d] = (s, d, 0.5, place(h, 2, -d), place(h, 2, 2), h, COL[d], [("g3", h, 2, d, d)])
    return plan


def scatter_plan():
    steps = {}
    for h in (0, 1):
        u, v = 1 - h, h

        def slot(uo, vo):
            return SLOT[(vo, uo) if h == 0 else (uo, vo)]

        for vo in (-1, 0, 1, 2):
            steps["A", h, vo] = (slot(2, vo), h, [], [(("A", h, vo, d), u, d, d) for d in (1, -1)])
            for d in (1, -1):
                steps["B", h, vo, d] = (
                    slot(d, vo), h, [(("A", h, vo, d), d)], [(("B", h, vo, d), u, d, 0)],
                )
        both = lambda vo: [(("B", h, vo, 1), 0), (("B", h, vo, -1), 0)]
        steps["D", h] = (slot(0, 2), h, both(2), [(("D", h, d), v, d, d) for d in (1, -1)])
        for d in (1, -1):
            steps["E", h, d] = (slot(0, d), h, both(d) + [(("D", h, d), d)], [(("E", h, d), v, d, 0)])
        steps["F", h] = (slot(0, 0), h, both(0) + [(("E", h, 1), 0), (("E", h, -1), 0)], [])
    return steps


def sequence():
    seq = []
    for i, (dx, dy) in enumerate(BLOCKS):
        seq.append(("G", i))
        if dy == 2:
            seq.append(("A", 0, dx))
        if dx == 2:
            seq.append(("A", 1, dy))
    for vo in (1, 2, -1):
        seq += [("B", h, vo, d) for h in (0, 1) for d in (1, -1)]
    seq += [("D", h) for h in (0, 1)]
    seq += [("B", h, 0, d) for h in (0, 1) for d in (1, -1)]
    seq += [("E", h, d) for h in (0, 1) for d in (1, -1)]
    return seq + [("F", h) for h in (0, 1)]


def schedule():
    gather, steps, seq = gather_plan(), scatter_plan(), sequence()
    pieces = {}
    for name, (_, _, _, _, target, _, _, _) in gather.items():
        pieces.setdefault(target, []).append(name)
    link, arrival, actions = {}, {}, []
    waited, issued, loaded, ready = set(), set(), {}, {}
    now = 0.0

    def send(name, axis, d, size):
        start = max(now, link.get((axis, d), 0.0))
        link[axis, d] = start + size * HALF_US
        arrival[name] = link[axis, d] + HOP_US

    def wait(name):
        if name not in waited:
            waited.add(name)
            actions.append(("wait", name))

    def here(names):
        return all(n in arrival and arrival[n] <= now for n in names)

    free = list(range(LOADS))
    stage = [(i, None) for i in range(STAGE)]
    last_gate = max(i for i, item in enumerate(seq) if item[0] == "G")
    at = 0
    done_gates = 0
    while at < len(seq):
        for name, (axis, d, size, _, _, _, _, needs) in gather.items():
            if name not in issued and here(needs):
                issued.add(name)
                for n in needs:
                    wait(n)
                actions.append(("gather", name))
                send(name, axis, d, size)
        for item in seq[at : at + 3]:
            if item in loaded:
                continue
            if item[0] == "G":
                need = pieces.get(item[1], [])
                if item[1] - done_gates > 1 or not here(need):
                    break
                for n in need:
                    wait(n)
                actions.append(("fetch", item[1]))
                loaded[item], ready[item] = [], now + LOAD_US
            else:
                loads = steps[item][2]
                if len(loads) > len(free) or not here([n for n, _ in loads]):
                    break
                taken = []
                for n, rows in loads:
                    wait(n)
                    r = free.pop(0)
                    taken.append((r, n, rows))
                    actions.append(("load", r, n, rows))
                loaded[item], ready[item] = taken, (now + LOAD_US if loads else now)
        item = seq[at]
        if item in loaded and ready[item] <= now:
            if item[0] == "G":
                actions.append(("gate", item[1]))
                now += GATE_US
                done_gates += 1
            else:
                slot, before = stage.pop(0)
                if before is not None:
                    for n in before:
                        now = max(now, arrival[n])
                        actions.append(("sent", n))
                actions.append(("down", item, slot, loaded[item]))
                now += DOWN_US
                free += [r for r, _, _ in loaded[item]]
                sends = steps[item][3]
                for n, axis, d, rows in sends:
                    send(n, axis, d, 0.5 if rows else 1.0)
                stage.append((slot, [n for n, _, _, _ in sends]))
            if at == last_gate:
                more = [(STAGE + i, None) for i in range(STAGE_MORE)]
                stage = more + stage
                free += list(range(LOADS, LOADS + 16 - STAGE_MORE))
            at += 1
            continue
        later = [t for t in arrival.values() if t > now] + [t for t in ready.values() if t > now]
        now = min(later)
    return actions, now, max(link.values())


def kernel(
    side, x_ref, wg_ref, wu_ref, wd_ref, y_ref, ag, ra, rb, rd, re,
    wg, wu, wd, hid, xbuf, rbuf, sbuf, gs, gr, ss, sr, ws, xs, ls, os,
):
    rows, dim = x_ref.shape
    ff = wg_ref.shape[1]
    half, wide = rows // 2, dim // 2
    me = lax.axis_index("tp")
    mx, my = me // side, lax.rem(me, side)

    def peer(axis, d):
        if axis == 0:
            return {"tp": lax.rem(mx + d + side, side) * side + my}
        return {"tp": mx * side + lax.rem(my + d + side, side)}

    barrier = pltpu.get_barrier_semaphore()
    for axis in (0, 1):
        for d in (1, -1):
            pl.semaphore_signal(barrier, inc=1, device_id=peer(axis, d), device_id_type=MESH)
    pl.semaphore_wait(barrier, 4)

    gather, steps = gather_plan(), scatter_plan()
    actions, _, _ = schedule()
    gather_id = {n: i for i, n in enumerate(gather)}
    scatter_id, scatter_send = {}, {}
    for item, (_, _, _, sends) in steps.items():
        for n, axis, d, part in sends:
            scatter_id[n] = len(scatter_id)
            scatter_send[n] = (axis, d, part)

    def span(part):
        return slice(None) if part == 0 else (pl.ds(0, half) if part == 1 else pl.ds(half, half))

    def landing(n):
        d = 0 if n[-1] == 1 else 1
        if n[0] == "A":
            return ra.at[n[1], d, n[2] % 4]
        if n[0] == "B":
            return rb.at[n[1], d, n[2] % 4]
        return (rd if n[0] == "D" else re).at[n[1], d]

    def piece(slot, h, col):
        source = x_ref if slot == 0 else ag.at[slot - 1]
        r = pl.ds(h * half, half)
        return source.at[r] if col is None else source.at[r, pl.ds(col * wide, wide)]

    def gather_copy(n):
        axis, d, _, source, target, h, col, _ = gather[n]
        return pltpu.make_async_remote_copy(
            src_ref=piece(source, h, col),
            dst_ref=piece(target, h, col),
            send_sem=gs.at[gather_id[n]],
            recv_sem=gr.at[gather_id[n]],
            device_id=peer(axis, d),
            device_id_type=MESH,
        )

    def stage_ref(slot):
        if slot < STAGE:
            return sbuf.at[slot]
        return spare(slot - STAGE)

    def spare(i):
        return (wg if i < 8 else wu).at[pl.ds((i % 8) * rows, rows)]

    def load_ref(r):
        return rbuf.at[r] if r < LOADS else spare(STAGE_MORE + r - LOADS)

    slot_of_send = {}

    def scatter_copy(n):
        axis, d, part = scatter_send[n]
        return pltpu.make_async_remote_copy(
            src_ref=stage_ref(slot_of_send[n]).at[span(part)],
            dst_ref=landing(n),
            send_sem=ss.at[scatter_id[n]],
            recv_sem=sr.at[scatter_id[n]],
            device_id=peer(axis, d),
            device_id_type=MESH,
        )

    def received(n):
        if n in gather:
            gather_copy(n).wait_recv()
        else:
            axis, d, part = scatter_send[n]
            pltpu.make_async_remote_copy(
                src_ref=landing(n),
                dst_ref=landing(n),
                send_sem=ss.at[scatter_id[n]],
                recv_sem=sr.at[scatter_id[n]],
                device_id=peer(axis, d),
                device_id_type=MESH,
            ).wait_recv()

    def load_copy(r, n, part):
        return pltpu.make_async_copy(landing(n), load_ref(r).at[span(part)], ls.at[r])

    def fetch_copy(slot, b):
        source = x_ref if slot == 0 else ag.at[slot - 1]
        return pltpu.make_async_copy(source, xbuf.at[b], xs.at[b])

    def gate(slot, b):
        pltpu.make_async_copy(x_ref, xbuf.at[b], xs.at[b]).wait()

        def tile(j, _):
            c = pl.ds(pl.multiple_of(j * TILE, TILE), TILE)
            g = jnp.dot(xbuf[b], wg[:, c], preferred_element_type=jnp.float32)
            u = jnp.dot(xbuf[b], wu[:, c], preferred_element_type=jnp.float32)
            hid[slot, :, c] = (jax.nn.gelu(g) * u).astype(jnp.bfloat16)
            return 0

        lax.fori_loop(0, ff // TILE, tile, 0)

    def down(item, stage, loads):
        slot, h, _, sends = steps[item]
        for r, n, part in loads:
            load_copy(r, n, part).wait()
        out = stage_ref(stage)

        def tile(j, _):
            c = pl.ds(pl.multiple_of(j * TILE, TILE), TILE)
            c_in = pl.ds(pl.multiple_of(h * wide + j * TILE, TILE), TILE)
            term = jnp.dot(hid[slot], wd[:, c_in], preferred_element_type=jnp.float32)
            for r, _, part in loads:
                if part == 0:
                    term = term + load_ref(r)[:, c].astype(jnp.float32)
            for at, rs in ((1, slice(0, half)), (-1, slice(half, rows))):
                piece_ = term[rs]
                for r, _, part in loads:
                    if part == at:
                        piece_ = piece_ + load_ref(r)[rs, c].astype(jnp.float32)
                out[rs, c] = piece_.astype(jnp.bfloat16)
            return 0

        lax.fori_loop(0, wide // TILE, tile, 0)
        if sends:
            for n, _, _, _ in sends:
                slot_of_send[n] = stage
                scatter_copy(n).start()
        else:
            result_copy(h, stage).start()

    def result_copy(h, stage):
        return pltpu.make_async_copy(stage_ref(stage), y_ref.at[:, pl.ds(h * wide, wide)], os.at[h])

    finished = set()
    result_stage = {}

    def run(action):
        kind = action[0]
        if kind == "wait":
            received(action[1])
        elif kind == "gather":
            gather_copy(action[1]).start()
        elif kind == "fetch":
            fetch_copy(action[1], action[1] % 2).start()
        elif kind == "load":
            load_copy(*action[1:]).start()
        elif kind == "sent":
            scatter_copy(action[1]).wait_send()
            finished.add(action[1])
        else:
            item, stage, loads = action[1:]
            if item[0] == "F":
                result_stage[item[1]] = stage
            down(item, stage, loads)

    before, rest = [[]], []
    for action in actions:
        if action[0] == "gate":
            before.append([])
        else:
            before[-1].append(action)
    rest = before.pop()

    weights = [
        pltpu.make_async_copy(a, b, ws.at[i])
        for i, (a, b) in enumerate(((wg_ref, wg), (wu_ref, wu), (wd_ref, wd)))
    ]
    for action in before[0]:
        run(action)
    for w in weights:
        w.start()
    for w in weights[:2]:
        w.wait()

    def step(s, _):
        for k, todo in enumerate(before):
            if k and todo:

                @pl.when(s == k)
                def _(todo=todo, k=k):
                    if k == 1:
                        weights[2].wait()
                    for action in todo:
                        run(action)

        gate(s, lax.rem(s, 2))
        return 0

    lax.fori_loop(0, len(before), step, 0)
    for action in rest:
        run(action)
    for n in gather:
        gather_copy(n).wait_send()
    for n in scatter_id:
        if n not in finished:
            scatter_copy(n).wait_send()
    for h in (0, 1):
        result_copy(h, result_stage[h]).wait()


def solution(mesh):
    side = math.isqrt(mesh.shape["tp"])

    def step(x, w_gate, w_up, w_down):
        rows, dim = x.shape
        ff = w_gate.shape[1]
        half, wide = rows // 2, dim // 2
        gathers = len(gather_plan())
        scatters = sum(len(s[3]) for s in scatter_plan().values())
        bf16 = jnp.bfloat16
        anywhere = pl.BlockSpec(memory_space=pl.ANY)
        shapes = [
            (rows, dim),
            (15, rows, dim),
            (2, 2, 4, half, wide),
            (2, 2, 4, rows, wide),
            (2, 2, half, wide),
            (2, 2, rows, wide),
        ]
        return pl.pallas_call(
            functools.partial(kernel, side),
            out_shape=[jax.ShapeDtypeStruct(shape, bf16) for shape in shapes],
            in_specs=[anywhere] * 4,
            out_specs=[anywhere] * len(shapes),
            scratch_shapes=[
                pltpu.VMEM((dim, ff), bf16),
                pltpu.VMEM((dim, ff), bf16),
                pltpu.VMEM((ff, dim), bf16),
                pltpu.VMEM((16, rows, ff), bf16),
                pltpu.VMEM((2, rows, dim), bf16),
                pltpu.VMEM((LOADS, rows, wide), bf16),
                pltpu.VMEM((STAGE, rows, wide), bf16),
                pltpu.SemaphoreType.DMA((gathers,)),
                pltpu.SemaphoreType.DMA((gathers,)),
                pltpu.SemaphoreType.DMA((scatters,)),
                pltpu.SemaphoreType.DMA((scatters,)),
                pltpu.SemaphoreType.DMA((3,)),
                pltpu.SemaphoreType.DMA((2,)),
                pltpu.SemaphoreType.DMA((LOADS + 16 - STAGE_MORE,)),
                pltpu.SemaphoreType.DMA((2,)),
            ],
            compiler_params=pltpu.CompilerParams(
                collective_id=0, has_side_effects=True, vmem_limit_bytes=66_000_000
            ),
        )(x, w_gate, w_up, w_down)[0]

    return jax.shard_map(
        step,
        mesh=mesh,
        in_specs=(P(("dp", "tp"), None), P(None, "tp"), P(None, "tp"), P("tp", None)),
        out_specs=P(("dp", "tp"), None),
        check_vma=False,
    )


if __name__ == "__main__":
    acts, end, links = schedule()
    for a in acts:
        print(a)
    print(len(acts), end, links)
```

time: 602 us -> 381 us (0.63)
  waiting for transfers between devices: 398 us -> 0 us
  Pallas kernels: 0 us -> 376 us
  matrix products: 190 us -> 0 us
  between operations: 13.4 us -> 0.01 us
    pallas_call x0 -> x1, Pallas kernels: none -> 376 us  [step(): pl.pallas_call(functools.partial(kernel, side), out_shape=[jax.ShapeDtype...]
    all_gather x1 -> x0, waiting for transfers between devices: 203 us -> none  [step(): rows = lax.all_gather(x, 'tp', axis=0, tiled=True)]
    reduce_scatter x1 -> x0, waiting for transfers between devices: 195 us -> none  [step(): return lax.psum_scatter(term, 'tp', scatter_dimension=0, tiled=True)]
    dot_general x3 -> x0, matrix products: 190 us -> none  [the longest x1 65.1 us: step(): up = jnp.dot(rows, w_up, preferred_element_type=jnp.float32)]
  transfers between devices with their start and end apart: 2 -> 0, of which waited for: 2 -> 0; matrix products, arithmetic and copies ran while one was open for 0% -> 0% of each run, Pallas kernels for 0% -> 0%
where the time goes in v1:
time: 381 us; the launch traced here: 379 us
  Pallas kernels  376 us (99%)
    pallas_call x1, Pallas kernels, step(): pl.pallas_call(functools.partial(kernel, side), out_shape=[jax.ShapeDtype...  376 us

profile of v1, /device:TPU:97, one launch (start us, length us, event | category | flops | bytes accessed | tf_op | source)
XLA Modules:
  0.0 379.3 jit_solution(17085965075218655361)
XLA Ops:
  0.0 376.2 %shard_map.46 = (bf16[352,3072]{1,0:T(8,128)(2,1)}, bf16[15,352,3072]{2,1,0:T(8,128)(2,1)}, bf16[2,2,4,176,1536]{4,3,2,1,0:T(8,128)(2,1)}, bf16[2,2,4,352,1536]{...) custom-call(bf16[352,3072]{1,0:T(8,128)(2,1)} %x_ref.1, ...), custom_call_target="tpu_custom_call" | custom-call | tf_op jit(solution)/shard_map/pallas_call | solution.py:418
  376.2 3.1 copy.6

commit v2 on v0

v2 whole, which is shorter than its diff:
```python
import functools
import math

import jax
import jax.numpy as jnp
from jax import lax
from jax.experimental import pallas as pl
from jax.experimental.pallas import tpu as pltpu
from jax.sharding import PartitionSpec as P

MESH = pl.DeviceIdType.MESH
TILE = 256
EARLY = 4
STAGE = 12
LOADS = 8

HALF_US, HOP_US, LOAD_US, DOWN_US, CORE_US = 23.4, 2.0, 2.0, 3.2, 2.0
GATE_US = (7.4, 2.5, 2.5, 2.5)

BLOCKS = [(0, 0), (0, 1), (0, -1), (0, 2), (2, 0), (2, 1), (2, -1), (2, 2)]
SLOT = {b: i for i, b in enumerate(BLOCKS)}
UNITS = [
    ((0, 1), (0, -1)), ((1, 1), (2, 1)), ((1, -1), (2, -1)), ((3, 1), (3, -1)),
    ((4, 1), (4, -1)), ((5, 1), (6, 1)), ((5, -1), (6, -1)), ((7, 1), (7, -1)),
]
GATES = [
    (0, 0, 5), (1, 0, 4), (0, 5, 6), (1, 4, 7), (2, 0, 1), (0, 6, 7), (2, 1, 8), (1, 7, 8),
    (0, 7, 8), (3, 0, 8),
]
STEPS = [
    ("A", 0, 2), ("B", 0, 0, -1), ("B", 0, 0, 1), ("X", 2), ("X", -1), ("B", 0, 2, -1),
    ("B", 0, 2, 1), ("A", 1, 2), ("X", 1), ("A", 1, 0), ("C", 0), ("A", 2, 0),
    ("X", 0), ("B", 1, 2, -1), ("B", 1, 2, 1), ("B", 2, 0, 1), ("B", 2, 0, -1), ("B", 1, 0, -1),
    ("C", 1), ("B", 1, 0, 1), ("F", 0), ("F", 2), ("F", 1),
]
EARLY_STEPS = [(("G", 3, 4), ("A", 0, 0))]
PIECE = 0.7273
ORDER = ("g1", "u1", "u2", "g2", "g3", "u3", "d0", "d2", "d1")


def transfers():
    plan = {}
    for d in (1, -1):
        plan["x1", d] = (0, d, 1.0, [], None)
        for part in (1, -1):
            plan["y1", 0, d, part] = (1, d, 1.0, [], None)
        plan["g1", d] = (0, d, PIECE, [], None)
    for d in (1, -1):
        plan["x2", d] = (0, d, 1.0, [("x1", d)], None)
        plan["y2", 0, d] = (1, d, 1.0, [("y1", 0, d, d)], None)
    for d in (1, -1):
        for w in ORDER[1:]:
            plan[w, d] = (0, d, PIECE, [], ("x2", d))
    for d in (1, -1):
        for w in ORDER:
            plan["over", w, d] = (2, 0, PIECE, [(w, d)], None)
        for part in (1, -1):
            plan["y1", 2, d, part] = (1, d, 1.0, [("x2", part)], None)
        plan["y2", 2, d] = (1, d, 1.0, [("y1", 2, d, d)], None)
        for t in (0, 1):
            plan["r2", t, 0, d] = (0, d, 1 / 3, [("r1", t, 0, d)], None)
        for dy in (2, 1, -1, 0):
            plan["r2", 2, dy, d] = (0, d, 1 / 3, [("r1", 2, dy, d)], None)
    return plan


def pieces_of(unit):
    names = []
    for slot, part in UNITS[unit]:
        across, dy = BLOCKS[slot]
        if dy == 0:
            names += [("x2", part)] if across else []
        elif dy == 2:
            names.append(("y2", across, part))
        else:
            names.append(("y1", across, -dy, part))
    return names


def weight_names(part):
    names = (f"g{part}", f"u{part}") if part < 4 else (f"d{part - 5}",)
    return [n for w in names for d in (1, -1) for n in ((w, d), ("over", w, d))]


def sums():
    steps = {}
    both = lambda t, e: [(("B", t, e, 1), 0), (("B", t, e, -1), 0)]
    over = lambda t, dy: [(("r2", t, dy, 1), 1), (("r2", t, dy, -1), -1)]
    for t in (0, 1):
        for e in (2, 0):
            steps["A", t, e] = (SLOT[e, 2], t, [], [(("A", t, e, d), 1, d, d) for d in (1, -1)])
            for d in (1, -1):
                steps["B", t, e, d] = (SLOT[e, d], t, [(("A", t, e, d), d)], [(("B", t, e, d), 1, d, 0)])
        steps["C", t] = (SLOT[2, 0], t, both(t, 2), [(("r1", t, 0, d), 0, d, d) for d in (1, -1)])
    for dy in (2, 1, -1, 0):
        steps["X", dy] = (SLOT[2, dy], 2, [], [(("r1", 2, dy, d), 0, d, d) for d in (1, -1)])
    steps["A", 2, 0] = (SLOT[0, 2], 2, over(2, 2), [(("A", 2, 0, d), 1, d, d) for d in (1, -1)])
    for d in (1, -1):
        loads = over(2, d) + [(("A", 2, 0, d), d)]
        steps["B", 2, 0, d] = (SLOT[0, d], 2, loads, [(("B", 2, 0, d), 1, d, 0)])
    for t in (0, 1, 2):
        steps["F", t] = (SLOT[0, 0], t, both(t, 0) + over(t, 0), [])
    return steps


def sequence():
    seq = [("G", part, i) for part, a, b in GATES for i in range(a, b)]
    for at, item in EARLY_STEPS:
        seq.insert(seq.index(at) + 1, item)
    return seq + STEPS


def schedule():
    plan, steps = transfers(), sums()
    seq = sequence()
    link, arrival, actions = {}, {}, []
    waited, issued, loaded, ready, brought = set(), set(), {}, {}, {}
    now = 0.0

    def send(name, axis, d, size):
        start = max(now, link.get((axis, d), 0.0))
        link[axis, d] = start + size * (CORE_US if axis == 2 else HALF_US)
        arrival[name] = link[axis, d] + HOP_US

    def wait(names):
        for name in names:
            if name not in waited:
                waited.add(name)
                actions.append(("wait", name))

    def here(names):
        return all(n in arrival and arrival[n] <= now for n in names)

    free = list(range(LOADS))
    stage = [(i, None) for i in range(EARLY)]
    own_left = sum(b - a for part, a, b in GATES if part == 0)
    gates = 1 + max(i for i, item in enumerate(seq) if item[0] == "G")
    at = fetched = 0
    while at < len(seq):
        for name, (axis, d, size, needs, after) in plan.items():
            if name not in issued and here(needs) and (after is None or after in issued):
                issued.add(name)
                wait(needs)
                actions.append(("go", name))
                send(name, axis, d, size)
        for part in (1, 2, 3, 4, 5, 6, 7):
            if part not in brought:
                names = [] if part == 4 else weight_names(part)
                if here(names) and not (part >= 4 and own_left):
                    wait(names)
                    actions.append(("bring", part))
                    brought[part] = now + 4.0
        for k, item in enumerate(seq[at : at + 3]):
            if item in loaded:
                continue
            if item[0] == "G":
                if k > 1 or not here(pieces_of(item[2])):
                    break
                wait(pieces_of(item[2]))
                actions.append(("fetch", item[2], fetched % 2))
                fetched += 1
                loaded[item], ready[item] = [], now + LOAD_US
            else:
                loads = steps[item][2]
                units = [i for i, u in enumerate(UNITS) if steps[item][0] in (u[0][0], u[1][0])]
                if any(("G", part, i) in seq[at:] for part in range(4) for i in units):
                    break
                if (loads and at < gates) or len(loads) > len(free) or not here([n for n, _ in loads]):
                    break
                wait([n for n, _ in loads])
                taken = []
                for n, rows in loads:
                    taken.append((free.pop(0), n, rows))
                    actions.append(("load", *taken[-1]))
                loaded[item], ready[item] = taken, (now + LOAD_US if loads else now)
        item = seq[at]
        parts = ([item[1]] if item[1] else []) if item[0] == "G" else [4, 5 + steps[item][1]]
        if item in loaded and ready[item] <= now and all(brought.get(q, 1e9) <= now for q in parts):
            if item[0] == "G":
                actions.append(("gate", item[1], item[2]))
                now += GATE_US[item[1]]
                own_left -= item[1] == 0
            else:
                slot, before = stage.pop(0)
                for n in before or []:
                    now = max(now, arrival[n])
                    actions.append(("sent", n))
                actions.append(("down", item, slot, loaded[item]))
                now += DOWN_US
                free += [r for r, _, _ in loaded[item]]
                for n, axis, d, rows in steps[item][3]:
                    send(n, axis, d, 1 / 3 if rows else 2 / 3)
                stage.append((slot, [n for n, _, _, _ in steps[item][3]]))
            at += 1
            if at == gates:
                stage = [(EARLY + i, None) for i in range(STAGE)] + stage
            continue
        now = min(t for t in [*arrival.values(), *ready.values(), *brought.values()] if t > now)
    return actions, now, max(link.values())


def kernel(
    side, x_ref, wg_ref, wu_ref, wd_ref, y_ref, ag, rl, nb, nd, ta, tb, rr, rf,
    w, hid, xbuf, sbuf, ts, tr, ss, sr, ws, xs, ls, os,
):
    rows, dim = x_ref.shape
    ff = wg_ref.shape[1]
    half, wide, third = rows // 2, dim // 2, dim // 3
    quarter = ff // 4
    some = quarter // 3
    me, group = lax.axis_index("tp"), lax.axis_index("dp")
    core = lax.rem(group, 2)
    mx, my = me // side, lax.rem(me, side)

    def peer(axis, d):
        if axis == 0:
            return {"tp": lax.rem(mx + d + side, side) * side + my}
        if axis == 1:
            return {"tp": mx * side + lax.rem(my + d + side, side)}
        return {"dp": group + 1 - 2 * core}

    barrier = pltpu.get_barrier_semaphore()
    for axis, d in ((0, 1), (0, -1), (1, 1), (1, -1), (2, 0)):
        pl.semaphore_signal(barrier, inc=1, device_id=peer(axis, d), device_id_type=MESH)
    pl.semaphore_wait(barrier, 5)

    plan, steps = transfers(), sums()
    actions, _, _ = schedule()
    plan_id = {n: i for i, n in enumerate(plan)}
    sum_id, sum_send = {}, {}
    for _, _, _, sends in steps.values():
        for n, axis, d, part in sends:
            sum_id[n] = len(sum_id)
            sum_send[n] = (axis, d, part)

    def way(d):
        return 0 if d == 1 else 1

    def span(part):
        return slice(None) if part == 0 else pl.ds(0 if part == 1 else half, half)

    def block(slot):
        return x_ref if slot == 0 else ag.at[slot - 1]

    def landing(n):
        d = way(n[-1])
        if n[0] == "A":
            return ta.at[n[1] * 2 + n[2] // 2, d]
        if n[0] == "B":
            return tb.at[n[1] * 2 + n[2] // 2, d]
        return (rr if n[0] == "r1" else rf).at[n[1] + n[2] % 4, d]

    def ends(n):
        kind, d = n[0], n[-1]
        if kind == "x1":
            return x_ref.at[span(d)], rl.at[way(d)]
        if kind == "x2":
            return rl.at[way(d)], block(SLOT[2, 0]).at[span(d)]
        if kind == "y1":
            _, e, d, part = n
            return block(SLOT[e, 0]).at[span(part)], block(SLOT[e, -d]).at[span(part)]
        if kind == "y2":
            e = n[1]
            return block(SLOT[e, -d]).at[span(d)], block(SLOT[e, 2]).at[span(d)]
        if kind == "r2":
            return landing(("r1", *n[1:])), landing(n)
        over = kind == "over"
        name = n[1] if over else kind
        number = int(name[1])
        if name[0] == "d":
            buf = nd.at[number, way(d)]
        else:
            buf = nb.at[number - 1, 0 if name[0] == "g" else 1, way(d)]
        if over:
            return buf.at[0], buf.at[1]
        at = (2 * quarter if d == 1 else 0) + quarter * core
        if name[0] == "d":
            start = pl.multiple_of(at, quarter)
            return wd_ref.at[pl.ds(start, quarter), pl.ds(number * third, third)], buf.at[0]
        start = pl.multiple_of(at + (number - 1) * some, some)
        return (wg_ref if name[0] == "g" else wu_ref).at[:, pl.ds(start, some)], buf.at[0]

    def moving(n):
        axis, d = plan[n][:2]
        source, target = ends(n)
        return pltpu.make_async_remote_copy(
            src_ref=source, dst_ref=target, send_sem=ts.at[plan_id[n]], recv_sem=tr.at[plan_id[n]],
            device_id=peer(axis, d), device_id_type=MESH,
        )

    def spare(i):
        if i < EARLY:
            return sbuf.at[i]
        i -= EARLY
        return w.at[2 + i // 8, pl.ds((i % 8) * rows, rows), pl.ds(0, third)]

    def load_ref(r):
        if r < 4:
            return spare(EARLY + STAGE + r)
        return xbuf.at[r // 2 - 2, :, pl.ds((r % 2) * wide, third)]

    slot_of = {}

    def leaving(n, source):
        axis, d, part = sum_send[n]
        return pltpu.make_async_remote_copy(
            src_ref=source, dst_ref=landing(n), send_sem=ss.at[sum_id[n]], recv_sem=sr.at[sum_id[n]],
            device_id=peer(axis, d), device_id_type=MESH,
        )

    def staged(n):
        return leaving(n, spare(slot_of[n]).at[span(sum_send[n][2])])

    def load_copy(r, n, part):
        return pltpu.make_async_copy(landing(n), load_ref(r).at[span(part)], ls.at[r])

    def bring(part):
        copies = []
        if part == 4:
            for h in (0, 1):
                copies.append((wd_ref.at[:, pl.ds(h * wide, wide)], w.at[0, pl.ds(h * ff, ff)]))
        elif part < 4:
            for p in range(4):
                for i in (0, 1):
                    target = w.at[2 + i, :, pl.ds(((part - 1) * 4 + p) * some, some)]
                    copies.append((nb.at[part - 1, i, p // 2, p % 2], target))
        else:
            t = part - 5
            for h in (0, 1):
                lo, hi = max(t * third, h * wide), min((t + 1) * third, (h + 1) * wide)
                if lo < hi:
                    for p in range(4):
                        source = nd.at[t, p // 2, p % 2, :, pl.ds(lo - t * third, hi - lo)]
                        target = w.at[1, pl.ds(h * ff + p * quarter, quarter), pl.ds(lo - h * wide, hi - lo)]
                        copies.append((source, target))
        base = {1: 2, 2: 10, 3: 18, 4: 26, 5: 28, 6: 32, 7: 40}[part]
        return [pltpu.make_async_copy(s, t, ws.at[base + i]) for i, (s, t) in enumerate(copies)]

    def gate_tiles(part, slot, b):
        pltpu.make_async_copy(x_ref, xbuf.at[b], xs.at[b]).wait()
        first, last = (0, ff // TILE) if part == 0 else (0, 4 * some // TILE)
        at = 2 if part else 0

        def pair(i, _):
            for j in (2 * i, 2 * i + 1):
                c = pl.ds(pl.multiple_of((4 * some * (part - 1) if part else 0) + j * TILE, TILE), TILE)
                g = jnp.dot(xbuf[b], w[at, :, c], preferred_element_type=jnp.float32)
                u = jnp.dot(xbuf[b], w[at + 1, :, c], preferred_element_type=jnp.float32)
                value = (jax.nn.gelu(g) * u).astype(jnp.bfloat16)
                for k in range(TILE // some):
                    start = j * TILE + k * some
                    if part:
                        start = (j * (TILE // some) + k) * quarter + (part - 1) * some
                    to = pl.ds(pl.multiple_of(start, some), some)
                    piece = value[:, k * some : (k + 1) * some]
                    hid[at // 2, slot, 0, :, to] = piece[:half]
                    hid[at // 2, slot, 1, :, to] = piece[half:]
            return 0

        lax.fori_loop(first // 2, last // 2, pair, 0)

    def down(item, stage, loads):
        slot, t, _, sends = steps[item]
        for r, n, part in loads:
            load_copy(r, n, part).wait()
        out = spare(stage)
        unit = [i for i, u in enumerate(UNITS) if slot in (u[0][0], u[1][0])]

        def hidden(i):
            if len(unit) == 1:
                return hid[i, unit[0]].reshape(rows, ff)
            which = [slot == UNITS[unit[0]][k][0] for k in (0, 1)].index(True)
            return hid[i, pl.ds(unit[0], 2), which].reshape(rows, ff)

        def tile(j, _):
            c = pl.ds(pl.multiple_of(j * TILE, TILE), TILE)
            at = t * third + j * TILE
            right = at // wide
            k = pl.ds(pl.multiple_of(right * ff, TILE), ff)
            c_in = pl.ds(pl.multiple_of(at - right * wide, TILE), TILE)
            term = jnp.dot(hidden(0), w[0, k, c_in], preferred_element_type=jnp.float32)
            term += jnp.dot(hidden(1), w[1, k, c_in], preferred_element_type=jnp.float32)
            for r, _, part in loads:
                if part == 0:
                    term = term + load_ref(r)[:, c].astype(jnp.float32)
            for side_, rs in ((1, slice(0, half)), (-1, slice(half, rows))):
                value = term[rs]
                for r, _, part in loads:
                    if part == side_:
                        value = value + load_ref(r)[rs, c].astype(jnp.float32)
                out[rs, c] = value.astype(jnp.bfloat16)
            return 0

        lax.fori_loop(0, third // TILE, tile, 0)
        for n, _, _, _ in sends:
            slot_of[n] = stage
            staged(n).start()
        if not sends:
            result_copy(t, stage).start()

    def result_copy(t, stage):
        return pltpu.make_async_copy(spare(stage), y_ref.at[:, pl.ds(t * third, third)], os.at[t])

    finished, result_stage, brought = set(), {}, set()

    def need(part):
        if part not in brought:
            brought.add(part)
            for copy in bring(part):
                copy.wait()

    def run(action):
        kind = action[0]
        if kind == "wait":
            n = action[1]
            (moving(n) if n in plan else leaving(n, landing(n))).wait_recv()
        elif kind == "go":
            moving(action[1]).start()
        elif kind == "fetch":
            b = action[2]
            (first, _), (second, part) = UNITS[action[1]]
            if first == second:
                pltpu.make_async_copy(block(first), xbuf.at[b], xs.at[b]).start()
            else:
                for slot, to in ((first, 1), (second, -1)):
                    source = block(slot).at[span(part)]
                    pltpu.make_async_copy(source, xbuf.at[b, span(to)], xs.at[b]).start()
        elif kind == "bring":
            for copy in bring(action[1]):
                copy.start()
        elif kind == "load":
            load_copy(*action[1:]).start()
        elif kind == "sent":
            staged(action[1]).wait_send()
            finished.add(action[1])
        else:
            item, stage, loads = action[1:]
            if item[0] == "F":
                result_stage[item[1]] = stage
            need(4)
            need(5 + steps[item][1])
            down(item, stage, loads)

    before, order = [[]], []
    for action in actions:
        if action[0] == "gate":
            before.append([])
            order.append(action)
        else:
            before[-1].append(action)
    rest = before.pop()

    own = [pltpu.make_async_copy(a, w.at[i], ws.at[i]) for i, a in enumerate((wg_ref, wu_ref))]
    for action in before[0]:
        run(action)
    for copy in own:
        copy.start()
    for copy in own:
        copy.wait()

    done = 0
    for part, a, b in GATES:
        if part and part not in brought:
            for action in before[done]:
                run(action)
            before[done] = []
            need(part)

        def step(s, _, part=part, a=a, done=done, b=b):
            for k in range(a, b):
                todo = before[done + k - a] if done + k - a else []
                if todo:

                    @pl.when(s == k)
                    def _(todo=todo):
                        for action in todo:
                            run(action)

            gate_tiles(part, s, lax.rem(s + (done - a), 2))
            return 0

        lax.fori_loop(a, b, step, 0)
        done += b - a
    for action in rest:
        run(action)
    for n in plan:
        moving(n).wait_send()
    for n in sum_id:
        if n not in finished:
            staged(n).wait_send()
    for t in (0, 1, 2):
        result_copy(t, result_stage[t]).wait()


def solution(mesh):
    side = math.isqrt(mesh.shape["tp"])

    def step(x, w_gate, w_up, w_down):
        rows, dim = x.shape
        ff = w_gate.shape[1]
        half, third, quarter = rows // 2, dim // 3, ff // 4
        moves = len(transfers())
        leaves = sum(len(s[3]) for s in sums().values())
        bf16 = jnp.bfloat16
        anywhere = pl.BlockSpec(memory_space=pl.ANY)
        shapes = [
            (rows, dim),
            (7, rows, dim),
            (2, half, dim),
            (3, 2, 2, 2, dim, quarter // 3),
            (3, 2, 2, quarter, third),
            (5, 2, half, third),
            (5, 2, rows, third),
            (6, 2, half, third),
            (6, 2, half, third),
        ]
        return pl.pallas_call(
            functools.partial(kernel, side),
            out_shape=[jax.ShapeDtypeStruct(shape, bf16) for shape in shapes],
            in_specs=[anywhere] * 4,
            out_specs=[anywhere] * len(shapes),
            scratch_shapes=[
                pltpu.VMEM((4, dim, ff), bf16),
                pltpu.VMEM((2, 8, 2, half, ff), bf16),
                pltpu.VMEM((2, rows, dim), bf16),
                pltpu.VMEM((EARLY, rows, third), bf16),
                pltpu.SemaphoreType.DMA((moves,)),
                pltpu.SemaphoreType.DMA((moves,)),
                pltpu.SemaphoreType.DMA((leaves,)),
                pltpu.SemaphoreType.DMA((leaves,)),
                pltpu.SemaphoreType.DMA((44,)),
                pltpu.SemaphoreType.DMA((2,)),
                pltpu.SemaphoreType.DMA((LOADS,)),
                pltpu.SemaphoreType.DMA((3,)),
            ],
            compiler_params=pltpu.CompilerParams(
                collective_id=0, has_side_effects=True, vmem_limit_bytes=66_900_000
            ),
        )(x, w_gate, w_up, w_down)[0]

    return jax.shard_map(
        step,
        mesh=mesh,
        in_specs=(P(("dp", "tp"), None), P(None, "tp"), P(None, "tp"), P("tp", None)),
        out_specs=P(("dp", "tp"), None),
        check_vma=False,
    )


if __name__ == "__main__":
    acts, end, links = schedule()
    for a in acts:
        print(a)
    print(len(acts), end, links)
```

time: 602 us -> 318 us (0.53)
  waiting for transfers between devices: 398 us -> 0 us
  Pallas kernels: 0 us -> 314 us
  matrix products: 190 us -> 0 us
  between operations: 13.4 us -> 0.01 us
    pallas_call x0 -> x1, Pallas kernels: none -> 314 us  [step(): pl.pallas_call(functools.partial(kernel, side), out_shape=[jax.ShapeDtype...]
    all_gather x1 -> x0, waiting for transfers between devices: 203 us -> none  [step(): rows = lax.all_gather(x, 'tp', axis=0, tiled=True)]
    reduce_scatter x1 -> x0, waiting for transfers between devices: 195 us -> none  [step(): return lax.psum_scatter(term, 'tp', scatter_dimension=0, tiled=True)]
    dot_general x3 -> x0, matrix products: 190 us -> none  [the longest x1 65.1 us: step(): up = jnp.dot(rows, w_up, preferred_element_type=jnp.float32)]
  transfers between devices with their start and end apart: 2 -> 0, of which waited for: 2 -> 0; matrix products, arithmetic and copies ran while one was open for 0% -> 0% of each run, Pallas kernels for 0% -> 0%
where the time goes in v2:
time: 318 us; the launch traced here: 317 us
  Pallas kernels  314 us (99%)
    pallas_call x1, Pallas kernels, step(): pl.pallas_call(functools.partial(kernel, side), out_shape=[jax.ShapeDtype...  314 us

profile of v2, /device:TPU:97, one launch (start us, length us, event | category | flops | bytes accessed | tf_op | source)
XLA Modules:
  0.0 317.3 jit_solution(17420824083606359922)
XLA Ops:
  0.0 314.2 %shard_map.46 = (bf16[352,3072]{1,0:T(8,128)(2,1)}, bf16[7,352,3072]{2,1,0:T(8,128)(2,1)}, bf16[2,176,3072]{2,1,0:T(8,128)(2,1)}, bf16[3,2,2,2,3072,128]{5,4,3,2...) custom-call(bf16[352,3072]{1,0:T(8,128)(2,1)} %x_ref.1, ...), custom_call_target="tpu_custom_call" | custom-call | tf_op jit(solution)/shard_map/pallas_call | solution.py:517
  314.2 3.1 copy.6

commit v3 on v2

--- a/solution.py
+++ b/solution.py
@@ -31,28 +31,30 @@
     ("A", 0, 2), ("B", 0, 0, -1), ("B", 0, 0, 1), ("X", 2), ("X", -1), ("B", 0, 2, -1),
     ("B", 0, 2, 1), ("A", 1, 2), ("X", 1), ("A", 1, 0), ("C", 0), ("A", 2, 0),
     ("X", 0), ("B", 1, 2, -1), ("B", 1, 2, 1), ("B", 2, 0, 1), ("B", 2, 0, -1), ("B", 1, 0, -1),
-    ("C", 1), ("B", 1, 0, 1), ("F", 0), ("F", 2), ("F", 1),
+    ("C", 1), ("B", 1, 0, 1), ("F", 0), ("F", 2), ("S",),
 ]
 EARLY_STEPS = [(("G", 3, 4), ("A", 0, 0))]
+LAST = 1
 PIECE = 0.7273
-ORDER = ("g1", "u1", "u2", "g2", "g3", "u3", "d0", "d2", "d1")
+ORDER = ("x1", "g1", "x2", "u1", "u2", "g2", "g3", "u3", "d0", "d2", "d1")
+WEIGHTS = [w for w in ORDER if w[0] != "x"]
 
 
 def transfers():
     plan = {}
+    for i, w in enumerate(ORDER):
+        for d in (1, -1):
+            if w == "x1":
+                plan["x1", d] = (0, d, 1.0, [], None)
+                for part in (1, -1):
+                    plan["y1", 0, d, part] = (1, d, 1.0, [], None)
+            elif w == "x2":
+                plan["x2", d] = (0, d, 1.0, [("x1", d)], None)
+                plan["y2", 0, d] = (1, d, 1.0, [("y1", 0, d, d)], None)
+            else:
+                plan[w, d] = (0, d, PIECE, [], ("x2", d) if "x2" in ORDER[:i] else None)
     for d in (1, -1):
-        plan["x1", d] = (0, d, 1.0, [], None)
-        for part in (1, -1):
-            plan["y1", 0, d, part] = (1, d, 1.0, [], None)
-        plan["g1", d] = (0, d, PIECE, [], None)
-    for d in (1, -1):
-        plan["x2", d] = (0, d, 1.0, [("x1", d)], None)
-        plan["y2", 0, d] = (1, d, 1.0, [("y1", 0, d, d)], None)
-    for d in (1, -1):
-        for w in ORDER[1:]:
-            plan[w, d] = (0, d, PIECE, [], ("x2", d))
-    for d in (1, -1):
-        for w in ORDER:
+        for w in WEIGHTS:
             plan["over", w, d] = (2, 0, PIECE, [(w, d)], None)
         for part in (1, -1):
             plan["y1", 2, d, part] = (1, d, 1.0, [("x2", part)], None)
@@ -98,7 +100,8 @@
     for d in (1, -1):
         loads = over(2, d) + [(("A", 2, 0, d), d)]
         steps["B", 2, 0, d] = (SLOT[0, d], 2, loads, [(("B", 2, 0, d), 1, d, 0)])
-    for t in (0, 1, 2):
+    steps["S",] = (SLOT[0, 0], LAST, [], [])
+    for t in {0, 1, 2} - {LAST}:
         steps["F", t] = (SLOT[0, 0], t, both(t, 0) + over(t, 0), [])
     return steps
 
@@ -181,7 +184,7 @@
                 now += GATE_US[item[1]]
                 own_left -= item[1] == 0
             else:
-                slot, before = stage.pop(0)
+                slot, before = stage.pop(0) if item[0] != "S" else (None, None)
                 for n in before or []:
                     now = max(now, arrival[n])
                     actions.append(("sent", n))
@@ -190,18 +193,30 @@
                 free += [r for r, _, _ in loaded[item]]
                 for n, axis, d, rows in steps[item][3]:
                     send(n, axis, d, 1 / 3 if rows else 2 / 3)
-                stage.append((slot, [n for n, _, _, _ in steps[item][3]]))
+                if item[0] != "S":
+                    stage.append((slot, [n for n, _, _, _ in steps[item][3]]))
             at += 1
             if at == gates:
                 stage = [(EARLY + i, None) for i in range(STAGE)] + stage
             continue
         now = min(t for t in [*arrival.values(), *ready.values(), *brought.values()] if t > now)
+    last = [(kind, LAST, 0, d) for kind in ("r2", "B") for d in (1, -1)]
+    while not here(last):
+        for name, (axis, d, size, needs, after) in plan.items():
+            if name not in issued and here(needs):
+                issued.add(name)
+                wait(needs)
+                actions.append(("go", name))
+                send(name, axis, d, size)
+        if not here(last):
+            now = min(t for t in arrival.values() if t > now)
+    wait(last)
     return actions, now, max(link.values())
 
 
 def kernel(
-    side, x_ref, wg_ref, wu_ref, wd_ref, y_ref, ag, rl, nb, nd, ta, tb, rr, rf,
-    w, hid, xbuf, sbuf, ts, tr, ss, sr, ws, xs, ls, os,
+    side, x_ref, wg_ref, wu_ref, wd_ref, y_ref, sum_ref, ag, rl, nb, nd, ta, tb, rr, rf,
+    w, hid, xbuf, sbuf, fbuf, ts, tr, ss, sr, ws, xs, ls, os,
 ):
     rows, dim = x_ref.shape
     ff = wg_ref.shape[1]
@@ -219,6 +234,9 @@
             return {"tp": mx * side + lax.rem(my + d + side, side)}
         return {"dp": group + 1 - 2 * core}
 
+    own = [pltpu.make_async_copy(a, w.at[i], ws.at[i]) for i, a in enumerate((wg_ref, wu_ref))]
+    for copy in own:
+        copy.start()
     barrier = pltpu.get_barrier_semaphore()
     for axis, d in ((0, 1), (0, -1), (1, 1), (1, -1), (2, 0)):
         pl.semaphore_signal(barrier, inc=1, device_id=peer(axis, d), device_id_type=MESH)
@@ -363,7 +381,7 @@
         slot, t, _, sends = steps[item]
         for r, n, part in loads:
             load_copy(r, n, part).wait()
-        out = spare(stage)
+        out = fbuf if stage is None else spare(stage)
         unit = [i for i, u in enumerate(UNITS) if slot in (u[0][0], u[1][0])]
 
         def hidden(i):
@@ -383,6 +401,9 @@
             for r, _, part in loads:
                 if part == 0:
                     term = term + load_ref(r)[:, c].astype(jnp.float32)
+            if stage is None:
+                out[:, c] = term
+                return 0
             for side_, rs in ((1, slice(0, half)), (-1, slice(half, rows))):
                 value = term[rs]
                 for r, _, part in loads:
@@ -399,6 +420,8 @@
             result_copy(t, stage).start()
 
     def result_copy(t, stage):
+        if stage is None:
+            return pltpu.make_async_copy(fbuf, sum_ref, os.at[t])
         return pltpu.make_async_copy(spare(stage), y_ref.at[:, pl.ds(t * third, third)], os.at[t])
 
     finished, result_stage, brought = set(), {}, set()
@@ -435,8 +458,8 @@
             finished.add(action[1])
         else:
             item, stage, loads = action[1:]
-            if item[0] == "F":
-                result_stage[item[1]] = stage
+            if item[0] in "FS":
+                result_stage[steps[item][1]] = stage
             need(4)
             need(5 + steps[item][1])
             down(item, stage, loads)
@@ -450,11 +473,8 @@
             before[-1].append(action)
     rest = before.pop()
 
-    own = [pltpu.make_async_copy(a, w.at[i], ws.at[i]) for i, a in enumerate((wg_ref, wu_ref))]
     for action in before[0]:
         run(action)
-    for copy in own:
-        copy.start()
     for copy in own:
         copy.wait()
 
@@ -490,6 +510,19 @@
             staged(n).wait_send()
     for t in (0, 1, 2):
         result_copy(t, result_stage[t]).wait()
+
+
+def finish(part_ref, sum_ref, along_ref, last_ref, y_ref):
+    third = sum_ref.shape[1]
+    for t in (0, 1, 2):
+        c = slice(t * third, (t + 1) * third)
+        if t == LAST:
+            value = sum_ref[...]
+            for piece in (along_ref[0, 0], along_ref[0, 1], last_ref[0, 0]):
+                value = value + piece.astype(jnp.float32)
+            y_ref[:, c] = value.astype(jnp.bfloat16)
+        else:
+            y_ref[:, c] = part_ref[:, c]
 
 
 def solution(mesh):
@@ -514,16 +547,19 @@
             (6, 2, half, third),
             (6, 2, half, third),
         ]
-        return pl.pallas_call(
+        kinds = [jax.ShapeDtypeStruct(shape, bf16) for shape in shapes]
+        kinds.insert(1, jax.ShapeDtypeStruct((rows, third), jnp.float32))
+        outs = pl.pallas_call(
             functools.partial(kernel, side),
-            out_shape=[jax.ShapeDtypeStruct(shape, bf16) for shape in shapes],
+            out_shape=kinds,
             in_specs=[anywhere] * 4,
-            out_specs=[anywhere] * len(shapes),
+            out_specs=[anywhere] * len(kinds),
             scratch_shapes=[
                 pltpu.VMEM((4, dim, ff), bf16),
                 pltpu.VMEM((2, 8, 2, half, ff), bf16),
                 pltpu.VMEM((2, rows, dim), bf16),
                 pltpu.VMEM((EARLY, rows, third), bf16),
+                pltpu.VMEM((rows, third), jnp.float32),
                 pltpu.SemaphoreType.DMA((moves,)),
                 pltpu.SemaphoreType.DMA((moves,)),
                 pltpu.SemaphoreType.DMA((leaves,)),
@@ -536,7 +572,19 @@
             compiler_params=pltpu.CompilerParams(
                 collective_id=0, has_side_effects=True, vmem_limit_bytes=66_900_000
             ),
-        )(x, w_gate, w_up, w_down)[0]
+        )(x, w_gate, w_up, w_down)
+        return pl.pallas_call(
+            finish,
+            grid=(2,),
+            out_shape=jax.ShapeDtypeStruct((rows, dim), bf16),
+            in_specs=[
+                pl.BlockSpec((half, dim), lambda k: (k, 0)),
+                pl.BlockSpec((half, third), lambda k: (k, 0)),
+                pl.BlockSpec((1, 2, half, third), lambda k: (2 * LAST, 0, k, 0)),
+                pl.BlockSpec((1, 1, half, third), lambda k: (LAST, k, 0, 0)),
+            ],
+            out_specs=pl.BlockSpec((half, dim), lambda k: (k, 0)),
+        )(outs[0], outs[1], outs[-3], outs[-1])
 
     return jax.shard_map(
         step,

time: 318 us -> 313 us (0.984)
    pallas_call x1 -> x2, Pallas kernels: 314 us -> 313 us  [the longest x1 309 us: step(): pl.pallas_call(functools.partial(kernel, side), out_shape=kinds, in_specs...]
where the time goes in v3:
time: 313 us
  Pallas kernels  313 us (100%)
    pallas_call x1, Pallas kernels, step(): pl.pallas_call(functools.partial(kernel, side), out_shape=kinds, in_specs...  309 us

profile of v3, /device:TPU:97, one launch (start us, length us, event | category | flops | bytes accessed | tf_op | source)
XLA Modules:
  0.0 312.8 jit_solution(5167657950463871751)
XLA Ops:
  0.0 308.9 %shard_map.46 = (bf16[352,3072]{1,0:T(8,128)(2,1)}, f32[352,1024]{1,0:T(8,128)}, bf16[7,352,3072]{2,1,0:T(8,128)(2,1)}, bf16[2,176,3072]{2,1,0:T(8,128)(2,1)}, b...) custom-call(bf16[352,3072]{1,0:T(8,128)(2,1)} %x_ref.1, ...), custom_call_target="tpu_custom_call" | custom-call | tf_op jit(solution)/shard_map/pallas_call | solution.py:552
  308.9 3.9 %shard_map.47 = bf16[352,3072]{1,0:T(8,128)(2,1)} custom-call(bf16[352,3072]{1,0:T(8,128)(2,1)} %get-tuple-element.9.part_ref, f32[352,1024]{1,0:T(8,128)} %get-tuple-element.10.sum_ref, bf16[5,2,352,1024]{3,2,1,0:T(8,128)(2,1)} %get-tuple-element.11.along_ref, bf16[6,2,176,1024]{3,2,1,0:T(8,128)(2,1)} %get-tuple-element.12.last_ref), custom_call_target="tpu_custom_call" | custom-call | tf_op jit(solution)/shard_map/pallas_call | solution.py:576

commit v4 on v3

--- a/solution.py
+++ b/solution.py
@@ -12,9 +12,10 @@
 TILE = 256
 EARLY = 4
 STAGE = 12
+EARLY_LOADS = 2
 LOADS = 8
 
-HALF_US, HOP_US, LOAD_US, DOWN_US, CORE_US = 23.4, 2.0, 2.0, 3.2, 2.0
+HALF_US, HOP_US, LOAD_US, DOWN_US, CORE_US = 23.3, 2.2, 2.0, 3.2, 2.0
 GATE_US = (7.4, 2.5, 2.5, 2.5)
 
 BLOCKS = [(0, 0), (0, 1), (0, -1), (0, 2), (2, 0), (2, 1), (2, -1), (2, 2)]
@@ -24,20 +25,23 @@
     ((4, 1), (4, -1)), ((5, 1), (6, 1)), ((5, -1), (6, -1)), ((7, 1), (7, -1)),
 ]
 GATES = [
-    (0, 0, 5), (1, 0, 4), (0, 5, 6), (1, 4, 7), (2, 0, 1), (0, 6, 7), (2, 1, 8), (1, 7, 8),
-    (0, 7, 8), (3, 0, 8),
+    (0, 0, 6), (2, 4, 1), (2, 6, 4), (1, 6, 4), (1, 0, 5), (2, 1, -1), (0, 7, 5), (2, 7, 8),
+    (1, 7, 8), (3, 7, -1),
 ]
 STEPS = [
-    ("A", 0, 2), ("B", 0, 0, -1), ("B", 0, 0, 1), ("X", 2), ("X", -1), ("B", 0, 2, -1),
-    ("B", 0, 2, 1), ("A", 1, 2), ("X", 1), ("A", 1, 0), ("C", 0), ("A", 2, 0),
-    ("X", 0), ("B", 1, 2, -1), ("B", 1, 2, 1), ("B", 2, 0, 1), ("B", 2, 0, -1), ("B", 1, 0, -1),
-    ("C", 1), ("B", 1, 0, 1), ("F", 0), ("F", 2), ("S",),
+    ("X", 1), ("A", 1, 0), ("X", -1), ("A", 2, 0), ("B", 1, 2, 1), ("B", 1, 2, -1),
+    ("X", 0), ("B", 0, 0, -1), ("B", 0, 0, 1), ("B", 2, 0, 1), ("C", 0), ("C", 1),
+    ("B", 2, 0, -1), ("B", 1, 0, 1), ("B", 1, 0, -1), ("F", 2), ("S",), ("F", 0),
 ]
-EARLY_STEPS = [(("G", 3, 4), ("A", 0, 0))]
+EARLY_STEPS = [(("G", 3, 7), ("A", 0, 2)), (("G", 3, 3), ("A", 0, 0)), (("A", 0, 0), ("B", 0, 2, -1)), (("B", 0, 2, -1), ("B", 0, 2, 1)), (("B", 0, 2, 1), ("X", 2)), (("G", 3, 1), ("A", 1, 2))]
 LAST = 1
 PIECE = 0.7273
-ORDER = ("x1", "g1", "x2", "u1", "u2", "g2", "g3", "u3", "d0", "d2", "d1")
+ORDER = ("x1", "g2", "x2", "u2", "u1", "g1", "g3", "u3", "d0", "d2", "d1")
 WEIGHTS = [w for w in ORDER if w[0] != "x"]
+
+
+def units_of(a, b):
+    return list(range(a, b, 1 if b > a else -1))
 
 
 def transfers():
@@ -107,7 +111,7 @@
 
 
 def sequence():
-    seq = [("G", part, i) for part, a, b in GATES for i in range(a, b)]
+    seq = [("G", part, i) for part, a, b in GATES for i in units_of(a, b)]
     for at, item in EARLY_STEPS:
         seq.insert(seq.index(at) + 1, item)
     return seq + STEPS
@@ -134,9 +138,9 @@
     def here(names):
         return all(n in arrival and arrival[n] <= now for n in names)
 
-    free = list(range(LOADS))
+    free = list(range(LOADS, LOADS + EARLY_LOADS))
     stage = [(i, None) for i in range(EARLY)]
-    own_left = sum(b - a for part, a, b in GATES if part == 0)
+    own_left = sum(abs(b - a) for part, a, b in GATES if part == 0)
     gates = 1 + max(i for i, item in enumerate(seq) if item[0] == "G")
     at = fetched = 0
     while at < len(seq):
@@ -168,7 +172,7 @@
                 units = [i for i, u in enumerate(UNITS) if steps[item][0] in (u[0][0], u[1][0])]
                 if any(("G", part, i) in seq[at:] for part in range(4) for i in units):
                     break
-                if (loads and at < gates) or len(loads) > len(free) or not here([n for n, _ in loads]):
+                if len(loads) > len(free) or not here([n for n, _ in loads]):
                     break
                 wait([n for n, _ in loads])
                 taken = []
@@ -198,6 +202,7 @@
             at += 1
             if at == gates:
                 stage = [(EARLY + i, None) for i in range(STAGE)] + stage
+                free = list(range(LOADS)) + free
             continue
         now = min(t for t in [*arrival.values(), *ready.values(), *brought.values()] if t > now)
     last = [(kind, LAST, 0, d) for kind in ("r2", "B") for d in (1, -1)]
@@ -216,7 +221,7 @@
 
 def kernel(
     side, x_ref, wg_ref, wu_ref, wd_ref, y_ref, sum_ref, ag, rl, nb, nd, ta, tb, rr, rf,
-    w, hid, xbuf, sbuf, fbuf, ts, tr, ss, sr, ws, xs, ls, os,
+    w, hid, xbuf, sbuf, fbuf, lbuf, ts, tr, ss, sr, ws, xs, ls, os,
 ):
     rows, dim = x_ref.shape
     ff = wg_ref.shape[1]
@@ -313,6 +318,8 @@
         return w.at[2 + i // 8, pl.ds((i % 8) * rows, rows), pl.ds(0, third)]
 
     def load_ref(r):
+        if r >= LOADS:
+            return lbuf.at[r - LOADS]
         if r < 4:
             return spare(EARLY + STAGE + r)
         return xbuf.at[r // 2 - 2, :, pl.ds((r % 2) * wide, third)]
@@ -487,8 +494,8 @@
             need(part)
 
         def step(s, _, part=part, a=a, done=done, b=b):
-            for k in range(a, b):
-                todo = before[done + k - a] if done + k - a else []
+            for k in range(abs(b - a)):
+                todo = before[done + k] if done + k else []
                 if todo:
 
                     @pl.when(s == k)
@@ -496,11 +503,11 @@
                         for action in todo:
                             run(action)
 
-            gate_tiles(part, s, lax.rem(s + (done - a), 2))
+            gate_tiles(part, a + s if b > a else a - s, lax.rem(s + done, 2))
             return 0
 
-        lax.fori_loop(a, b, step, 0)
-        done += b - a
+        lax.fori_loop(0, abs(b - a), step, 0)
+        done += abs(b - a)
     for action in rest:
         run(action)
     for n in plan:
@@ -560,13 +567,14 @@
                 pltpu.VMEM((2, rows, dim), bf16),
                 pltpu.VMEM((EARLY, rows, third), bf16),
                 pltpu.VMEM((rows, third), jnp.float32),
+                pltpu.VMEM((EARLY_LOADS, rows, third), bf16),
                 pltpu.SemaphoreType.DMA((moves,)),
                 pltpu.SemaphoreType.DMA((moves,)),
                 pltpu.SemaphoreType.DMA((leaves,)),
                 pltpu.SemaphoreType.DMA((leaves,)),
                 pltpu.SemaphoreType.DMA((44,)),
                 pltpu.SemaphoreType.DMA((2,)),
-                pltpu.SemaphoreType.DMA((LOADS,)),
+                pltpu.SemaphoreType.DMA((LOADS + EARLY_LOADS,)),
                 pltpu.SemaphoreType.DMA((3,)),
             ],
             compiler_params=pltpu.CompilerParams(

time: 313 us -> 314 us (level)
  no operation moved by 1% of the time
where the time goes in v4:
time: 314 us
  Pallas kernels  314 us (100%)
    pallas_call x1, Pallas kernels, step(): pl.pallas_call(functools.partial(kernel, side), out_shape=kinds, in_specs...  310 us

profile of v4, /device:TPU:97, one launch (start us, length us, event | category | flops | bytes accessed | tf_op | source)
XLA Modules:
  0.0 313.9 jit_solution(6132265764998949526)
XLA Ops:
  0.0 310.0 %shard_map.46 = (bf16[352,3072]{1,0:T(8,128)(2,1)}, f32[352,1024]{1,0:T(8,128)}, bf16[7,352,3072]{2,1,0:T(8,128)(2,1)}, bf16[2,176,3072]{2,1,0:T(8,128)(2,1)}, b...) custom-call(bf16[352,3072]{1,0:T(8,128)(2,1)} %x_ref.1, ...), custom_call_target="tpu_custom_call" | custom-call | tf_op jit(solution)/shard_map/pallas_call | solution.py:559
  310.0 3.9 %shard_map.47 = bf16[352,3072]{1,0:T(8,128)(2,1)} custom-call(bf16[352,3072]{1,0:T(8,128)(2,1)} %get-tuple-element.9.part_ref, f32[352,1024]{1,0:T(8,128)} %get-tuple-element.10.sum_ref, bf16[5,2,352,1024]{3,2,1,0:T(8,128)(2,1)} %get-tuple-element.11.along_ref, bf16[6,2,176,1024]{3,2,1,0:T(8,128)(2,1)} %get-tuple-element.12.last_ref), custom_call_target="tpu_custom_call" | custom-call | tf_op jit(solution)/shard_map/pallas_call | solution.py:584
